TPU v7x, 128 devices: a whole 4x4x4 slice. The times are simulated.
128 devices in a mesh: dim: 16 (over y, x), batch: 8 (over z, core).
Axes of the slice: x: 4, y: 4, z: 4, core: 2. Of those that a mesh axis runs over, the one named last changes fastest.
Arguments:
- start: float32 [2048, 4096], P('batch', 'dim'), may hold values from -6 to 6
- increments: float32 [3, 2048, 4096], P(None, 'batch', 'dim'), may hold values from -0.75 to 0.75
- w_in: bfloat16 [4096, 4096], P(None, 'dim'), may hold values from -0.09375 to 0.09375
- w_out: bfloat16 [4096, 4096], P('dim'), may hold values from -0.09375 to 0.09375
- initial: float32 [], replicated, may hold values from 4 to 5.5
Outputs:
- residual: float32 [2048], P('batch')
- grad_in: float32 [4096, 4096], P('batch', 'dim')
- grad_out: float32 [4096, 4096], P('dim', 'batch')
All inputs are finite; a program needn't handle non-finite values.
Results may differ from a plain program's by a relative error of at most 0.0051.
Values may be sent and summed in bfloat16 or wider, within the bound.
A program may use at most 128 MiB of HBM per device.

v0:
```python
import math
import jax
import jax.numpy as jnp
from jax import lax
from jax.sharding import Mesh
from jax.sharding import PartitionSpec as P

D = 4096
STEPS = 3
DIM = ("y", "x")
BATCH = ("z", "c")
time_step = 1.0 / 64.0
lam_coef = 50.0
noise_coef = math.sqrt(2.0)


def a2a(array, axis):
    return lax.all_to_all(array, axis, split_axis=0, concat_axis=0, tiled=True)


def scatter_sum(parts, axis):
    got = a2a(parts.astype(jnp.bfloat16), axis)
    return jnp.sum(got.astype(jnp.float32), 0)


def on_device(start, increments, w_in, w_out, initial):
    zscale = 2.0 / math.sqrt(D)
    rows, width = start.shape
    f32, bf16 = (jnp.float32, jnp.bfloat16)
    win = a2a(w_in.reshape(4, 4, width, width).transpose(1, 0, 2, 3), "x")
    wout = a2a(w_out.reshape(width, 4, 4, width).transpose(2, 1, 0, 3), "x")
    states = [start]
    for step in range(STEPS):
        states.append(states[-1] + noise_coef * increments[step])
    xb = jnp.stack(states[:STEPS]).astype(bf16).reshape(STEPS * rows, width)
    inc = increments.reshape(STEPS * rows, width)
    xg = lax.all_gather(xb, "y")
    h = scatter_sum(jnp.einsum("jrd,ijdh->irh", xg, win, preferred_element_type=f32), "x")
    act = jax.nn.silu(h).astype(bf16)
    ag = lax.all_gather(act, "x")
    z = zscale * scatter_sum(jnp.einsum("irh,ijhd->jrd", ag, wout, preferred_element_type=f32), "y")
    terms = jnp.sum(
        (0.5 * lam_coef * time_step * z * z + z * inc).reshape(STEPS, rows, width), (0, 2)
    )
    norm = jnp.sum(states[STEPS] * states[STEPS], 1)
    both = lax.psum(jnp.stack([terms, norm]), DIM)
    residual = initial + both[0] - jnp.log((1.0 + both[1]) * 0.5)
    scale = jnp.tile(zscale * residual, STEPS)[:, None]
    gz = (scale * (lam_coef * time_step * z + inc)).astype(bf16)
    gg = lax.all_gather(gz, "y")
    ga = scatter_sum(jnp.einsum("jrd,ijhd->irh", gg, wout, preferred_element_type=f32), "x")
    sig = jax.nn.sigmoid(h)
    gh = (ga * sig * (1.0 + h * (1.0 - sig))).astype(bf16)
    hg = lax.all_gather(gh, "x")
    gout = jnp.einsum("irh,jrd->jihd", ag, gg, preferred_element_type=f32)
    gin = jnp.einsum("jrd,irh->jidh", xg, hg, preferred_element_type=f32)
    grads = jnp.stack([gin, gout], 1)
    grads = grads.reshape(4, 2, 2, 2, width, width).transpose(3, 0, 1, 2, 4, 5)
    grads = lax.psum_scatter(grads.reshape(2, 4, -1), "c", scatter_dimension=0, tiled=False)
    grads = scatter_sum(grads, "z").reshape(2, 2, width, width)
    grads = lax.all_gather(grads, "c")
    grads = grads.transpose(2, 0, 1, 3, 4).reshape(4, -1)
    grads = a2a(grads.astype(bf16), "x").astype(f32).reshape(2, 2, 2, width, width)
    mine = lax.dynamic_index_in_dim(grads, lax.axis_index("c"), 0, keepdims=False)
    return (
        residual,
        mine[:, 0].reshape(2 * width, width),
        mine[:, 1].transpose(1, 0, 2).reshape(width, 2 * width),
    )


def solution(mesh):
    finer = Mesh(mesh.devices.reshape(4, 4, 4, 2), ("y", "x", "z", "c"))
    return jax.shard_map(
        on_device,
        mesh=finer,
        in_specs=(P(BATCH, DIM), P(None, BATCH, DIM), P(None, DIM), P(DIM, None), P()),
        out_specs=(P(BATCH), P(BATCH, DIM), P(DIM, BATCH)),
        check_vma=False,
    )
```

profile of v0, /device:TPU:1, one launch (start us, length us, event | category | flops | bytes accessed | tf_op | source)
XLA Modules:
  0.0 433.0 jit_solution(6734123639831771158)
XLA Ops:
  7.2 0.0 all-gather.6.cloned.1.call-start
  7.2 1.6 convert_bitcast_fusion.2
  8.8 0.8 pad_maximum_fusion
  9.6 0.0 all-gather.6.cloned.1.call-update
  9.6 0.0 all-gather.8.cloned.1.call-start
  9.7 0.1 copy.66
  9.8 30.1 %all_to_all.37 = bf16[4,4,256,256]{3,2,1,0:T(8,128)(2,1)S(1)} all-to-all(bf16[4,4,256,256]{3,2,1,0:T(8,128)(2,1)S(1)} %bitcast.164), channel_id=1, replica_groups=mesh['y'=4,'x'=4,'z'=4,'c'=2] {'x'}, dimensions={0} | all-to-all | bytes 4194304 | tf_op jit(solution)/shard_map/all_to_all | solution.py:18
  39.9 3.2 fusion.10
  43.1 23.3 %all_to_all.38 = bf16[4,768,256]{2,1,0:T(8,128)(2,1)S(1)} all-to-all(bf16[4,768,256]{2,1,0:T(8,128)(2,1)S(1)} %fusion.10), channel_id=1, replica_groups=mesh['y'=4,'x'=4,'z'=4,'c'=2] {'x'}, dimensions={0} | all-to-all | bytes 3145728 | tf_op jit(solution)/shard_map/all_to_all | solution.py:18
  66.4 0.2 convert_reduce_fusion.3
  66.7 1.0 fusion.26
  67.7 0.5 copy-done.2
  68.2 2.5 copy.43
  70.6 2.8 copy.44
  73.4 40.7 %all_to_all.39 = bf16[4,4,256,256]{3,2,1,0:T(8,128)(2,1)} all-to-all(bf16[4,4,256,256]{3,2,1,0:T(8,128)(2,1)S(1)} %copy.44), channel_id=1, replica_groups=mesh['y'=4,'x'=4,'z'=4,'c'=2] {'x'}, dimensions={0} | all-to-all | bytes 4194304 | tf_op jit(solution)/shard_map/all_to_all | solution.py:18
  114.1 1.5 all-gather.8.cloned.1.call-done
  115.6 5.1 %fusion.16 = bf16[4,768,256]{2,1,0:T(8,128)(2,1)} fusion(bf16[4,4,256,256]{3,2,1,0:T(8,128)(2,1)} %all_to_all.39, bf16[4,768,256]{2,1,0:T(8,128)(2,1)} %all-gather.8.cloned.1.call-done), kind=kOutput, calls=%fused_computation.23 | convolution fusion | flops 1611399168 | bytes 5242880 | tf_op jit(solution)/shard_map/irh,ijhd->jrd/dot_general | solution.py:41
  120.7 4.3 %all-to-all-start.3 = ((bf16[4,768,256]{2,1,0:T(8,128)(2,1)}), bf16[4,768,256]{2,1,0:T(8,128)(2,1)}, u32[]{:S(2)}, u32[]{:S(2)}) async-start(bf16[4,768,256]{2,1,0:T(8,128)(2,1)} %fusion.16), calls=%async_computation.3 | async-start | bytes 3145728 | tf_op jit(solution)/shard_map/all_to_all | solution.py:18
  125.1 0.0 all-gather.10.cloned.1.call-start
  125.8 19.2 %all-to-all-done.3 = bf16[4,768,256]{2,1,0:T(8,128)(2,1)} async-done(((bf16[4,768,256]{2,1,0:T(8,128)(2,1)}), bf16[4,768,256]{2,1,0:T(8,128)(2,1)}, u32[]{:S(2)}, u32[]{:S(2)}) %all-to-all-start.3) | async-done | bytes 1572896 | tf_op jit(solution)/shard_map/all_to_all | solution.py:18
  145.0 1.7 convert_reduce_fusion.2
  146.7 0.1 broadcast_multiply_fusion.1
  146.9 0.2 multiply_reduce_fusion
  147.1 28.5 %psum.7 = f32[2,256]{1,0:T(2,128)S(1)} all-reduce(f32[2,256]{1,0:T(2,128)S(1)} %pad_maximum_fusion.1), channel_id=1, replica_groups=mesh['y'=4,'x'=4,'z'=4,'c'=2] {'y','x'}, use_global_device_ids=true, to_apply=%region_4.5 | all-reduce | flops 512 | bytes 4096 | tf_op jit(solution)/shard_map/psum | solution.py:46
  175.6 0.6 broadcast_multiply_fusion.2
  176.2 0.9 fusion.22
  177.1 0.0 all-gather.12.cloned.1.call-start
  177.2 31.8 %all-gather.10.cloned.1.call-done = bf16[4,768,256]{2,1,0:T(8,128)(2,1)} async-done(((bf16[1,768,256]{2,1,0:T(8,128)(2,1)}), bf16[4,768,256]{2,1,0:T(8,128)(2,1)}) %all-gather.10.cloned.1.call-update) | async-done | bytes 1572880 | tf_op jit(solution)/shard_map/all_gather | solution.py:50
  209.0 3.9 fusion.13
  212.9 23.5 %all_to_all.40 = bf16[4,768,256]{2,1,0:T(8,128)(2,1)S(1)} all-to-all(bf16[4,768,256]{2,1,0:T(8,128)(2,1)S(1)} %fusion.13), channel_id=1, replica_groups=mesh['y'=4,'x'=4,'z'=4,'c'=2] {'x'}, dimensions={0} | all-to-all | bytes 3145728 | tf_op jit(solution)/shard_map/all_to_all | solution.py:18
  236.3 0.2 convert_reduce_fusion.1
  236.6 1.0 fusion.20
  237.6 0.5 all-gather.14.cloned.1.call-start
  238.1 0.6 dynamic-slice
  238.7 5.2 %fusion.2 = f32[4,256,4,256]{3,1,2,0:T(8,128)} fusion(bf16[4,768,256]{2,1,0:T(8,128)(2,1)} %all-gather.10.cloned.1.call-done, bf16[4,768,256]{2,1,0:T(8,128)(2,1)S(1)} %copy-done.4), kind=kOutput, calls=%fused_computation.13 | convolution fusion | flops 1610612736 | bytes 7340032 | tf_op jit(solution)/shard_map/irh,jrd->jihd/dot_general | solution.py:55
  243.9 5.4 %copy.49 = f32[4,1,2,2,256,256]{5,4,2,1,0,3:T(8,128)} copy(f32[4,1,2,2,256,256]{4,5,3,2,0,1:T(8,128)} %bitcast.168) | data formatting | bytes 8388608 | tf_op jit(solution)/shard_map/stack | solution.py:57
  249.3 13.9 %all-gather.12.cloned.1.call-done = bf16[4,768,256]{2,1,0:T(8,128)(2,1)} async-done(((bf16[1,768,256]{2,1,0:T(8,128)(2,1)}), bf16[4,768,256]{2,1,0:T(8,128)(2,1)}) %all-gather.12.cloned.1.call-update) | async-done | bytes 1572880 | tf_op jit(solution)/shard_map/all_gather | solution.py:54
  263.2 5.2 %fusion.4 = f32[4,256,4,256]{3,1,2,0:T(8,128)} fusion(bf16[4,768,256]{2,1,0:T(8,128)(2,1)} %all-gather.12.cloned.1.call-done, bf16[4,768,256]{2,1,0:T(8,128)(2,1)S(1)} %copy-done.3), kind=kOutput, calls=%fused_computation.15 | convolution fusion | flops 1610612736 | bytes 7340032 | tf_op jit(solution)/shard_map/jrd,irh->jidh/dot_general | solution.py:56
  268.4 5.3 %copy.48 = f32[4,1,2,2,256,256]{5,4,2,1,0,3:T(8,128)} copy(f32[4,1,2,2,256,256]{4,5,0,3,2,1:T(8,128)} %bitcast.169) | data formatting | bytes 8388608 | tf_op jit(solution)/shard_map/stack | solution.py:57
  273.6 7.6 %maximum_bitcast_fusion = f32[2,4,2,2,256,256]{5,4,3,2,1,0:T(8,128)} fusion(f32[4,1,2,2,256,256]{5,4,2,1,0,3:T(8,128)} %copy.49, f32[4,1,2,2,256,256]{5,4,2,1,0,3:T(8,128)} %copy.48), kind=kLoop, calls=%fused_computation | loop fusion | flops 2097152 | bytes 16777216 | tf_op jit(solution)/shard_map/transpose | solution.py:58
  281.2 8.4 %reshape.194 = f32[2,4,262144]{2,1,0:T(4,128)} reshape(f32[2,4,2,2,256,256]{5,4,3,2,1,0:T(8,128)} %maximum_bitcast_fusion) | data formatting | bytes 16777216 | tf_op jit(solution)/shard_map/reshape | solution.py:59
  289.6 26.2 %all-reduce.2 = bf16[2,4,262144]{2,1,0:T(4,128)(2,1)} all-reduce(f32[2,4,262144]{2,1,0:T(4,128)} %reshape.194), channel_id=2, replica_groups=mesh['y'=4,'x'=4,'z'=4,'c'=2] {'c'}, use_global_device_ids=true, to_apply=%region_6.7.clone | all-reduce | flops 2097152 | bytes 12582912
  315.7 2.6 fusion
  318.4 0.5 broadcast.101
  318.9 4.6 %reduce.3 = bf16[4,262144]{1,0:T(4,128)(2,1)} reduce(bf16[4,1,262144]{2,0,1:T(4,128)(2,1)S(1)} %fusion, bf16[]{:T(256)} %broadcast.101), dimensions={1}, to_apply=%copy.50.reduce_sub_computation | reduce | bytes 4194306 | tf_op jit(solution)/shard_map/convert_element_type | solution.py:22
  323.5 5.0 %reshape.207 = bf16[4,2,131072]{2,1,0:T(2,128)(2,1)} reshape(bf16[4,262144]{1,0:T(4,128)(2,1)} %reduce.3) | data formatting | bytes 4194304
  328.5 30.3 %all_to_all.41 = bf16[4,2,131072]{2,1,0:T(2,128)(2,1)S(1)} all-to-all(bf16[4,2,131072]{2,1,0:T(2,128)(2,1)} %reshape.207), channel_id=1, replica_groups=mesh['y'=4,'x'=4,'z'=4,'c'=2] {'z'}, dimensions={0} | all-to-all | bytes 4194304 | tf_op jit(solution)/shard_map/all_to_all | solution.py:18
  358.8 3.4 reshape.208
  362.2 11.9 %convert_reduce_fusion = bf16[262144]{0:T(1024)(128)(2,1)S(1)} fusion(bf16[4,1,262144]{2,1,0:T(2,128)(2,1)} %reshape.208), kind=kLoop, calls=%fused_computation.2 | loop fusion | flops 1835008 | bytes 2621440 | tf_op jit(solution)/shard_map/reduce_sum | solution.py:23
  374.1 1.0 all_gather_reshape.4
  375.1 10.9 %all-gather.14.cloned.1.call-done = bf16[2,2,2,256,256]{4,3,2,1,0:T(8,128)(2,1)} async-done(((bf16[1,2,2,256,256]{4,3,2,1,0:T(8,128)(2,1)}), bf16[2,2,2,256,256]{4,3,2,1,0:T(8,128)(2,1)}) %all-gather.14.cloned.1.call-update) | async-done | bytes 1048592 | tf_op jit(solution)/shard_map/all_gather | solution.py:61
  386.0 1.3 copy.51
  387.3 0.5 convert_element_type.130
  387.8 7.4 %reduce.4 = bf16[4,131072]{1,0:T(4,128)(2,1)S(1)} reduce(bf16[4,1,131072]{2,1,0:T(2,128)(2,1)S(1)} %convert_element_type.130, bf16[]{:T(256)} %broadcast.101), dimensions={1}, to_apply=%convert_element_type.130.reduce_sub_computation | reduce | bytes 2097154 | tf_op jit(solution)/shard_map/convert_element_type | solution.py:63
  395.2 2.0 reshape.209
  397.3 4.3 all-to-all-start.6
  401.6 14.7 %all-to-all-done.6 = bf16[4,2,65536]{2,1,0:T(2,128)(2,1)S(1)} async-done(((bf16[4,2,65536]{2,1,0:T(2,128)(2,1)}), bf16[4,2,65536]{2,1,0:T(2,128)(2,1)S(1)}, u32[]{:S(2)}, u32[]{:S(2)}) %all-to-all-start.6) | async-done | bytes 1048608 | tf_op jit(solution)/shard_map/all_to_all | solution.py:18
  416.2 0.9 reshape.210
  417.2 6.4 %convert_reduce_fusion.4 = f32[4,131072]{1,0:T(4,128)S(1)} fusion(bf16[4,1,131072]{2,1,0:T(2,128)(2,1)S(1)} %reshape.210), kind=kLoop, calls=%fused_computation.11 | loop fusion | flops 524288 | bytes 3145728 | tf_op jit(solution)/shard_map/convert_element_type | solution.py:63
  423.6 0.4 copy.64
  424.0 0.1 dynamic-slice_bitcast_fusion
  424.1 0.9 slice_bitcast_fusion
  425.0 0.2 copy.53
  425.2 1.0 copy.54
  (19 shorter events, 0.1 us)
Async XLA Ops:
  7.2 2.5 copy-start.1
  7.2 32.7 %all-gather.6.cloned.1.call-start = ((), (), s32[]{:S(2)}) async-start(), calls=%async_computation.7 | async-start | bytes 1966080 | tf_op jit(solution)/shard_map/all_gather | solution.py:37
  9.6 106.0 %all-gather.8.cloned.1.call-start = ((), (), s32[]{:S(2)}) async-start(), calls=%async_computation.8 | async-start | bytes 1966080 | tf_op jit(solution)/shard_map/all_gather | solution.py:40
  66.4 1.7 copy-start.2
  120.7 24.3 %all-to-all-start.3 = ((bf16[4,768,256]{2,1,0:T(8,128)(2,1)}), bf16[4,768,256]{2,1,0:T(8,128)(2,1)}, u32[]{:S(2)}, u32[]{:S(2)}) async-start(bf16[4,768,256]{2,1,0:T(8,128)(2,1)} %fusion.16), calls=%async_computation.3 | async-start | bytes 3145728 | tf_op jit(solution)/shard_map/all_to_all | solution.py:18
  125.1 83.9 %all-gather.10.cloned.1.call-start = ((), (), s32[]{:S(2)}) async-start(), calls=%async_computation.9 | async-start | bytes 1966080 | tf_op jit(solution)/shard_map/all_gather | solution.py:50
  125.8 21.1 %copy-start = (f32[3,256,256]{2,1,0:T(8,128)S(1)}, f32[3,256,256]{2,1,0:T(8,128)}, u32[]{:S(2)}) copy-start(f32[3,256,256]{2,1,0:T(8,128)} %param.6) | copy-start | bytes 2359300
  177.1 86.1 %all-gather.12.cloned.1.call-start = ((), (), s32[]{:S(2)}) async-start(), calls=%async_computation.10 | async-start | bytes 1966080 | tf_op jit(solution)/shard_map/all_gather | solution.py:54
  236.3 1.8 copy-start.5
  236.3 2.4 copy-start.4
  237.6 148.4 %all-gather.14.cloned.1.call-start = ((), (), s32[]{:S(2)}) async-start(), calls=%async_computation.11 | async-start | bytes 1572864 | tf_op jit(solution)/shard_map/all_gather | solution.py:61
  243.9 19.3 %copy-start.3 = (bf16[4,768,256]{2,1,0:T(8,128)(2,1)S(1)}, bf16[4,768,256]{2,1,0:T(8,128)(2,1)}, u32[]{:S(2)}) copy-start(bf16[4,768,256]{2,1,0:T(8,128)(2,1)} %all-gather.6.cloned.1.call-done) | copy-start | bytes 4718596
  397.3 19.0 %all-to-all-start.6 = ((bf16[4,2,65536]{2,1,0:T(2,128)(2,1)}), bf16[4,2,65536]{2,1,0:T(2,128)(2,1)S(1)}, u32[]{:S(2)}, u32[]{:S(2)}) async-start(bf16[4,2,65536]{2,1,0:T(2,128)(2,1)} %reshape.209), calls=%async_computation.6 | async-start | bytes 2097152 | tf_op jit(solution)/shard_map/all_to_all | solution.py:18
Sparse Core Ops, SparseCore 0:
  10.2 29.4 all-gather.5
  67.8 47.8 all-gather.7
  177.2 31.6 all-gather.9
  237.7 25.4 all-gather.11
  375.2 10.7 all-gather.13
where the time goes:
time: 439 us; the launch traced here: 433 us
  blocking collectives  203 us (46%)
  waiting for transfers between devices  92.2 us (21%)
  other arithmetic  46.3 us (11%)
  local copies, waits for them, and re-layouts  45.3 us (10%)
  matrix products  22.5 us (5%)
  between operations  14.9 us (3%)
  starting transfers between devices  9.29 us (2%)
    all_to_all x5, blocking collectives, a2a(): return lax.all_to_all(array, axis, split_axis=0, concat_axis=0, tiled=True)  148 us
    all_to_all x2, waiting for transfers between devices, a2a(): return lax.all_to_all(array, axis, split_axis=0, concat_axis=0, tiled=True)  33.9 us
    all_gather x1, waiting for transfers between devices, on_device(): gg = lax.all_gather(gz, 'y')  31.8 us
    psum x1, blocking collectives, on_device(): both = lax.psum(jnp.stack([terms, norm]), DIM)  28.5 us
    unnamed x1, blocking collectives  26.2 us
    unnamed x20, local copies, waits for them, and re-layouts  16.3 us
    reduce_sum x4, other arithmetic, scatter_sum(): return jnp.sum(got.astype(jnp.float32), 0)  14.1 us
    all_gather x1, waiting for transfers between devices, on_device(): hg = lax.all_gather(gh, 'x')  13.9 us
  transfers between devices with their start and end apart: 7, of which 6 were waited for; matrix products, arithmetic and copies ran while one was open for 4% of the time, Pallas kernels for 0%

commit v1 on v0

--- a/solution.py
+++ b/solution.py
@@ -43,7 +43,7 @@
         (0.5 * lam_coef * time_step * z * z + z * inc).reshape(STEPS, rows, width), (0, 2)
     )
     norm = jnp.sum(states[STEPS] * states[STEPS], 1)
-    both = lax.psum(jnp.stack([terms, norm]), DIM)
+    both = lax.psum(lax.psum(jnp.stack([terms, norm]), "y"), "x")
     residual = initial + both[0] - jnp.log((1.0 + both[1]) * 0.5)
     scale = jnp.tile(zscale * residual, STEPS)[:, None]
     gz = (scale * (lam_coef * time_step * z + inc)).astype(bf16)

time: 439 us -> 421 us (0.959)
  blocking collectives: 203 us -> 187 us
    psum x1 -> x2, blocking collectives: 28.5 us -> 12.9 us  [on_device(): both = lax.psum(lax.psum(jnp.stack([terms, norm]), 'y'), 'x')]
where the time goes in v1:
time: 421 us; the launch traced here: 414 us
  blocking collectives  187 us (44%)
  waiting for transfers between devices  89.3 us (21%)
  other arithmetic  46.3 us (11%)
  local copies, waits for them, and re-layouts  45.3 us (11%)
  matrix products  22.5 us (5%)
  between operations  14.9 us (4%)
  starting transfers between devices  9.29 us (2%)
    all_to_all x5, blocking collectives, a2a(): return lax.all_to_all(array, axis, split_axis=0, concat_axis=0, tiled=True)  148 us
    all_to_all x2, waiting for transfers between devices, a2a(): return lax.all_to_all(array, axis, split_axis=0, concat_axis=0, tiled=True)  33.9 us
    all_gather x1, waiting for transfers between devices, on_device(): gg = lax.all_gather(gz, 'y')  28.9 us
    unnamed x1, blocking collectives  26.2 us
    unnamed x20, local copies, waits for them, and re-layouts  16.3 us
    reduce_sum x4, other arithmetic, scatter_sum(): return jnp.sum(got.astype(jnp.float32), 0)  14.1 us
    all_gather x1, waiting for transfers between devices, on_device(): hg = lax.all_gather(gh, 'x')  13.9 us
    psum x2, blocking collectives, on_device(): both = lax.psum(lax.psum(jnp.stack([terms, norm]), 'y'), 'x')  12.9 us
  transfers between devices with their start and end apart: 7, of which 6 were waited for; matrix products, arithmetic and copies ran while one was open for 4% of the time, Pallas kernels for 0%

profile of v1, /device:TPU:1, one launch (start us, length us, event | category | flops | bytes accessed | tf_op | source)
XLA Modules:
  0.0 414.4 jit_solution(2776035961903867730)
XLA Ops:
  7.2 0.0 all-gather.6.cloned.1.call-start
  7.2 1.6 convert_bitcast_fusion.2
  8.8 0.8 pad_maximum_fusion
  9.6 0.0 all-gather.8.cloned.1.call-start
  9.7 0.1 copy.66
  9.8 30.1 %all_to_all.37 = bf16[4,4,256,256]{3,2,1,0:T(8,128)(2,1)S(1)} all-to-all(bf16[4,4,256,256]{3,2,1,0:T(8,128)(2,1)S(1)} %bitcast.164), channel_id=1, replica_groups=mesh['y'=4,'x'=4,'z'=4,'c'=2] {'x'}, dimensions={0} | all-to-all | bytes 4194304 | tf_op jit(solution)/shard_map/all_to_all | solution.py:18
  39.9 3.2 fusion.10
  43.1 23.3 %all_to_all.38 = bf16[4,768,256]{2,1,0:T(8,128)(2,1)S(1)} all-to-all(bf16[4,768,256]{2,1,0:T(8,128)(2,1)S(1)} %fusion.10), channel_id=1, replica_groups=mesh['y'=4,'x'=4,'z'=4,'c'=2] {'x'}, dimensions={0} | all-to-all | bytes 3145728 | tf_op jit(solution)/shard_map/all_to_all | solution.py:18
  66.4 0.2 convert_reduce_fusion.3
  66.7 1.0 fusion.26
  67.7 0.5 copy-done.2
  68.2 2.5 copy.43
  70.6 2.8 copy.44
  73.4 40.7 %all_to_all.39 = bf16[4,4,256,256]{3,2,1,0:T(8,128)(2,1)} all-to-all(bf16[4,4,256,256]{3,2,1,0:T(8,128)(2,1)S(1)} %copy.44), channel_id=1, replica_groups=mesh['y'=4,'x'=4,'z'=4,'c'=2] {'x'}, dimensions={0} | all-to-all | bytes 4194304 | tf_op jit(solution)/shard_map/all_to_all | solution.py:18
  114.1 1.5 all-gather.8.cloned.1.call-done
  115.6 5.1 %fusion.16 = bf16[4,768,256]{2,1,0:T(8,128)(2,1)} fusion(bf16[4,4,256,256]{3,2,1,0:T(8,128)(2,1)} %all_to_all.39, bf16[4,768,256]{2,1,0:T(8,128)(2,1)} %all-gather.8.cloned.1.call-done), kind=kOutput, calls=%fused_computation.23 | convolution fusion | flops 1611399168 | bytes 5242880 | tf_op jit(solution)/shard_map/irh,ijhd->jrd/dot_general | solution.py:41
  120.7 4.3 %all-to-all-start.3 = ((bf16[4,768,256]{2,1,0:T(8,128)(2,1)}), bf16[4,768,256]{2,1,0:T(8,128)(2,1)}, u32[]{:S(2)}, u32[]{:S(2)}) async-start(bf16[4,768,256]{2,1,0:T(8,128)(2,1)} %fusion.16), calls=%async_computation.3 | async-start | bytes 3145728 | tf_op jit(solution)/shard_map/all_to_all | solution.py:18
  125.1 0.0 all-gather.10.cloned.1.call-start
  125.8 19.2 %all-to-all-done.3 = bf16[4,768,256]{2,1,0:T(8,128)(2,1)} async-done(((bf16[4,768,256]{2,1,0:T(8,128)(2,1)}), bf16[4,768,256]{2,1,0:T(8,128)(2,1)}, u32[]{:S(2)}, u32[]{:S(2)}) %all-to-all-start.3) | async-done | bytes 1572896 | tf_op jit(solution)/shard_map/all_to_all | solution.py:18
  145.0 1.7 convert_reduce_fusion.2
  146.7 0.1 broadcast_multiply_fusion.1
  146.9 0.2 multiply_reduce_fusion
  147.1 6.9 %psum.14 = f32[2,256]{1,0:T(2,128)S(1)} all-reduce(f32[2,256]{1,0:T(2,128)S(1)} %pad_maximum_fusion.1), channel_id=1, replica_groups=mesh['y'=4,'x'=4,'z'=4,'c'=2] {'y'}, use_global_device_ids=true, to_apply=%region_4.5 | all-reduce | flops 512 | bytes 4096 | tf_op jit(solution)/shard_map/psum | solution.py:46
  153.9 6.0 %psum.15 = f32[2,256]{1,0:T(2,128)S(1)} all-reduce(f32[2,256]{1,0:T(2,128)S(1)} %psum.14), channel_id=1, replica_groups=mesh['y'=4,'x'=4,'z'=4,'c'=2] {'x'}, use_global_device_ids=true, to_apply=%region_5.6 | all-reduce | flops 512 | bytes 4096 | tf_op jit(solution)/shard_map/psum | solution.py:46
  159.9 0.6 broadcast_multiply_fusion.2
  160.5 0.9 fusion.22
  161.5 0.0 all-gather.12.cloned.1.call-start
  161.5 28.9 %all-gather.10.cloned.1.call-done = bf16[4,768,256]{2,1,0:T(8,128)(2,1)} async-done(((bf16[1,768,256]{2,1,0:T(8,128)(2,1)}), bf16[4,768,256]{2,1,0:T(8,128)(2,1)}) %all-gather.10.cloned.1.call-update) | async-done | bytes 1572880 | tf_op jit(solution)/shard_map/all_gather | solution.py:50
  190.4 3.9 fusion.13
  194.3 23.5 %all_to_all.40 = bf16[4,768,256]{2,1,0:T(8,128)(2,1)S(1)} all-to-all(bf16[4,768,256]{2,1,0:T(8,128)(2,1)S(1)} %fusion.13), channel_id=1, replica_groups=mesh['y'=4,'x'=4,'z'=4,'c'=2] {'x'}, dimensions={0} | all-to-all | bytes 3145728 | tf_op jit(solution)/shard_map/all_to_all | solution.py:18
  217.8 0.2 convert_reduce_fusion.1
  218.0 1.0 fusion.20
  219.1 0.5 all-gather.14.cloned.1.call-start
  219.6 0.6 dynamic-slice
  220.2 5.2 %fusion.2 = f32[4,256,4,256]{3,1,2,0:T(8,128)} fusion(bf16[4,768,256]{2,1,0:T(8,128)(2,1)} %all-gather.10.cloned.1.call-done, bf16[4,768,256]{2,1,0:T(8,128)(2,1)S(1)} %copy-done.4), kind=kOutput, calls=%fused_computation.13 | convolution fusion | flops 1610612736 | bytes 7340032 | tf_op jit(solution)/shard_map/irh,jrd->jihd/dot_general | solution.py:55
  225.4 5.4 %copy.49 = f32[4,1,2,2,256,256]{5,4,2,1,0,3:T(8,128)} copy(f32[4,1,2,2,256,256]{4,5,3,2,0,1:T(8,128)} %bitcast.168) | data formatting | bytes 8388608 | tf_op jit(solution)/shard_map/stack | solution.py:57
  230.8 13.9 %all-gather.12.cloned.1.call-done = bf16[4,768,256]{2,1,0:T(8,128)(2,1)} async-done(((bf16[1,768,256]{2,1,0:T(8,128)(2,1)}), bf16[4,768,256]{2,1,0:T(8,128)(2,1)}) %all-gather.12.cloned.1.call-update) | async-done | bytes 1572880 | tf_op jit(solution)/shard_map/all_gather | solution.py:54
  244.7 5.2 %fusion.4 = f32[4,256,4,256]{3,1,2,0:T(8,128)} fusion(bf16[4,768,256]{2,1,0:T(8,128)(2,1)} %all-gather.12.cloned.1.call-done, bf16[4,768,256]{2,1,0:T(8,128)(2,1)S(1)} %copy-done.3), kind=kOutput, calls=%fused_computation.15 | convolution fusion | flops 1610612736 | bytes 7340032 | tf_op jit(solution)/shard_map/jrd,irh->jidh/dot_general | solution.py:56
  249.8 5.3 %copy.48 = f32[4,1,2,2,256,256]{5,4,2,1,0,3:T(8,128)} copy(f32[4,1,2,2,256,256]{4,5,0,3,2,1:T(8,128)} %bitcast.169) | data formatting | bytes 8388608 | tf_op jit(solution)/shard_map/stack | solution.py:57
  255.1 7.6 %maximum_bitcast_fusion = f32[2,4,2,2,256,256]{5,4,3,2,1,0:T(8,128)} fusion(f32[4,1,2,2,256,256]{5,4,2,1,0,3:T(8,128)} %copy.49, f32[4,1,2,2,256,256]{5,4,2,1,0,3:T(8,128)} %copy.48), kind=kLoop, calls=%fused_computation | loop fusion | flops 2097152 | bytes 16777216 | tf_op jit(solution)/shard_map/transpose | solution.py:58
  262.7 8.4 %reshape.194 = f32[2,4,262144]{2,1,0:T(4,128)} reshape(f32[2,4,2,2,256,256]{5,4,3,2,1,0:T(8,128)} %maximum_bitcast_fusion) | data formatting | bytes 16777216 | tf_op jit(solution)/shard_map/reshape | solution.py:59
  271.0 26.2 %all-reduce.2 = bf16[2,4,262144]{2,1,0:T(4,128)(2,1)} all-reduce(f32[2,4,262144]{2,1,0:T(4,128)} %reshape.194), channel_id=2, replica_groups=mesh['y'=4,'x'=4,'z'=4,'c'=2] {'c'}, use_global_device_ids=true, to_apply=%region_7.8.clone | all-reduce | flops 2097152 | bytes 12582912
  297.2 2.6 fusion
  299.8 0.5 broadcast.101
  300.4 4.6 %reduce.3 = bf16[4,262144]{1,0:T(4,128)(2,1)} reduce(bf16[4,1,262144]{2,0,1:T(4,128)(2,1)S(1)} %fusion, bf16[]{:T(256)} %broadcast.101), dimensions={1}, to_apply=%copy.50.reduce_sub_computation | reduce | bytes 4194306 | tf_op jit(solution)/shard_map/convert_element_type | solution.py:22
  305.0 5.0 %reshape.207 = bf16[4,2,131072]{2,1,0:T(2,128)(2,1)} reshape(bf16[4,262144]{1,0:T(4,128)(2,1)} %reduce.3) | data formatting | bytes 4194304
  310.0 30.3 %all_to_all.41 = bf16[4,2,131072]{2,1,0:T(2,128)(2,1)S(1)} all-to-all(bf16[4,2,131072]{2,1,0:T(2,128)(2,1)} %reshape.207), channel_id=1, replica_groups=mesh['y'=4,'x'=4,'z'=4,'c'=2] {'z'}, dimensions={0} | all-to-all | bytes 4194304 | tf_op jit(solution)/shard_map/all_to_all | solution.py:18
  340.3 3.4 reshape.208
  343.6 11.9 %convert_reduce_fusion = bf16[262144]{0:T(1024)(128)(2,1)S(1)} fusion(bf16[4,1,262144]{2,1,0:T(2,128)(2,1)} %reshape.208), kind=kLoop, calls=%fused_computation.2 | loop fusion | flops 1835008 | bytes 2621440 | tf_op jit(solution)/shard_map/reduce_sum | solution.py:23
  355.6 1.0 all_gather_reshape.4
  356.6 10.9 %all-gather.14.cloned.1.call-done = bf16[2,2,2,256,256]{4,3,2,1,0:T(8,128)(2,1)} async-done(((bf16[1,2,2,256,256]{4,3,2,1,0:T(8,128)(2,1)}), bf16[2,2,2,256,256]{4,3,2,1,0:T(8,128)(2,1)}) %all-gather.14.cloned.1.call-update) | async-done | bytes 1048592 | tf_op jit(solution)/shard_map/all_gather | solution.py:61
  367.5 1.3 copy.51
  368.8 0.5 convert_element_type.130
  369.3 7.4 %reduce.4 = bf16[4,131072]{1,0:T(4,128)(2,1)S(1)} reduce(bf16[4,1,131072]{2,1,0:T(2,128)(2,1)S(1)} %convert_element_type.130, bf16[]{:T(256)} %broadcast.101), dimensions={1}, to_apply=%convert_element_type.130.reduce_sub_computation | reduce | bytes 2097154 | tf_op jit(solution)/shard_map/convert_element_type | solution.py:63
  376.7 2.0 reshape.209
  378.7 4.3 %all-to-all-start.6 = ((bf16[4,2,65536]{2,1,0:T(2,128)(2,1)}), bf16[4,2,65536]{2,1,0:T(2,128)(2,1)S(1)}, u32[]{:S(2)}, u32[]{:S(2)}) async-start(bf16[4,2,65536]{2,1,0:T(2,128)(2,1)} %reshape.209), calls=%async_computation.6 | async-start | bytes 2097152 | tf_op jit(solution)/shard_map/all_to_all | solution.py:18
  383.0 14.7 %all-to-all-done.6 = bf16[4,2,65536]{2,1,0:T(2,128)(2,1)S(1)} async-done(((bf16[4,2,65536]{2,1,0:T(2,128)(2,1)}), bf16[4,2,65536]{2,1,0:T(2,128)(2,1)S(1)}, u32[]{:S(2)}, u32[]{:S(2)}) %all-to-all-start.6) | async-done | bytes 1048608 | tf_op jit(solution)/shard_map/all_to_all | solution.py:18
  397.7 0.9 reshape.210
  398.7 6.4 %convert_reduce_fusion.4 = f32[4,131072]{1,0:T(4,128)S(1)} fusion(bf16[4,1,131072]{2,1,0:T(2,128)(2,1)S(1)} %reshape.210), kind=kLoop, calls=%fused_computation.11 | loop fusion | flops 524288 | bytes 3145728 | tf_op jit(solution)/shard_map/convert_element_type | solution.py:63
  405.1 0.4 copy.64
  405.5 0.1 dynamic-slice_bitcast_fusion
  405.6 0.9 slice_bitcast_fusion
  406.5 0.2 copy.53
  406.7 1.0 copy.54
  (20 shorter events, 0.1 us)
Async XLA Ops:
  7.2 2.5 copy-start.1
  7.2 32.7 %all-gather.6.cloned.1.call-start = ((), (), s32[]{:S(2)}) async-start(), calls=%async_computation.7 | async-start | bytes 1966080 | tf_op jit(solution)/shard_map/all_gather | solution.py:37
  9.6 106.0 %all-gather.8.cloned.1.call-start = ((), (), s32[]{:S(2)}) async-start(), calls=%async_computation.8 | async-start | bytes 1966080 | tf_op jit(solution)/shard_map/all_gather | solution.py:40
  66.4 1.7 copy-start.2
  120.7 24.3 %all-to-all-start.3 = ((bf16[4,768,256]{2,1,0:T(8,128)(2,1)}), bf16[4,768,256]{2,1,0:T(8,128)(2,1)}, u32[]{:S(2)}, u32[]{:S(2)}) async-start(bf16[4,768,256]{2,1,0:T(8,128)(2,1)} %fusion.16), calls=%async_computation.3 | async-start | bytes 3145728 | tf_op jit(solution)/shard_map/all_to_all | solution.py:18
  125.1 65.3 %all-gather.10.cloned.1.call-start = ((), (), s32[]{:S(2)}) async-start(), calls=%async_computation.9 | async-start | bytes 1966080 | tf_op jit(solution)/shard_map/all_gather | solution.py:50
  125.8 21.1 %copy-start = (f32[3,256,256]{2,1,0:T(8,128)S(1)}, f32[3,256,256]{2,1,0:T(8,128)}, u32[]{:S(2)}) copy-start(f32[3,256,256]{2,1,0:T(8,128)} %param.6) | copy-start | bytes 2359300
  161.5 83.2 %all-gather.12.cloned.1.call-start = ((), (), s32[]{:S(2)}) async-start(), calls=%async_computation.10 | async-start | bytes 1966080 | tf_op jit(solution)/shard_map/all_gather | solution.py:54
  217.8 1.8 copy-start.5
  217.8 2.4 copy-start.4
  219.1 148.4 %all-gather.14.cloned.1.call-start = ((), (), s32[]{:S(2)}) async-start(), calls=%async_computation.11 | async-start | bytes 1572864 | tf_op jit(solution)/shard_map/all_gather | solution.py:61
  225.3 19.3 %copy-start.3 = (bf16[4,768,256]{2,1,0:T(8,128)(2,1)S(1)}, bf16[4,768,256]{2,1,0:T(8,128)(2,1)}, u32[]{:S(2)}) copy-start(bf16[4,768,256]{2,1,0:T(8,128)(2,1)} %all-gather.6.cloned.1.call-done) | copy-start | bytes 4718596
  378.7 19.0 %all-to-all-start.6 = ((bf16[4,2,65536]{2,1,0:T(2,128)(2,1)}), bf16[4,2,65536]{2,1,0:T(2,128)(2,1)S(1)}, u32[]{:S(2)}, u32[]{:S(2)}) async-start(bf16[4,2,65536]{2,1,0:T(2,128)(2,1)} %reshape.209), calls=%async_computation.6 | async-start | bytes 2097152 | tf_op jit(solution)/shard_map/all_to_all | solution.py:18
Sparse Core Ops, SparseCore 0:
  10.2 29.4 all-gather.5
  67.8 47.8 all-gather.7
  161.6 28.7 all-gather.9
  219.2 25.4 all-gather.11
  356.7 10.7 all-gather.13
